TPU v7x, 128 devices: a whole 4x4x4 slice. The times are simulated.
128 devices in a mesh: dp: 8 (over z, core), sp: 16 (over y, x).
Axes of the slice: x: 4, y: 4, z: 4, core: 2. Of those that a mesh axis runs over, the one named last changes fastest.
Arguments:
- queries_in: bfloat16 [16, 16384, 16, 128], P('dp', 'sp'), may hold values from -6 to 6
- keys_in: bfloat16 [16, 16384, 16, 128], P('dp', 'sp'), may hold values from -6 to 6
- values_in: bfloat16 [16, 16384, 16, 128], P('dp', 'sp'), may hold values from -6 to 6
- out_weight: bfloat16 [2048, 2048], P('dp'), may hold values from -0.125 to 0.125
Outputs:
- block_out: bfloat16 [16, 16384, 2048], P('dp', 'sp')
All inputs are finite; a program needn't handle non-finite values.
Results may differ from a plain program's by a relative error of at most 0.006.
Values may be sent and summed in bfloat16 or wider, within the bound.
A program may use at most 320 MiB of HBM per device.

v0:
```python
import jax
import jax.numpy as jnp
from jax import lax
from jax.sharding import PartitionSpec as P


def together(arrays, axis):
    ends = [0]
    for a in arrays:
        ends.append(ends[-1] + a.size)
    so_far = lax.psum(jnp.concatenate([a.ravel() for a in arrays]), axis)
    return tuple((so_far[b:e].reshape(a.shape) for a, b, e in zip(arrays, ends, ends[1:])))


def feature_map(values):
    wide = values.astype(jnp.float32)
    return (wide * wide + 0.1).astype(jnp.bfloat16)


def finish_heads(read, count):
    result = read * count**0.5
    return result.astype(jnp.bfloat16)


def look_up(features, state, mass):
    top = jnp.einsum(
        "bthd,bhde->bthe", features, state.astype(jnp.bfloat16), preferred_element_type=jnp.float32
    )
    bottom = jnp.einsum("bthd,bhd->bth", features.astype(jnp.float32), mass)
    return top / (bottom + 0.001)[..., None]


def on_device(queries_in, keys_in, values_in, out_weight):
    query_feature, key_feature = (feature_map(queries_in), feature_map(keys_in))
    count = queries_in.shape[1] * lax.axis_size("sp")
    part_state = jnp.einsum(
        "bthd,bthe->bhde", key_feature, values_in, preferred_element_type=jnp.float32
    )
    part_mass = jnp.sum(key_feature.astype(jnp.float32), axis=1)
    state, mass = together((part_state, part_mass), "sp")
    read = look_up(query_feature, state / count, mass / count)
    mixed = finish_heads(read, count)
    mixed = mixed.reshape(mixed.shape[0], mixed.shape[1], -1)
    return jnp.einsum(
        "btw,wv->btv",
        mixed,
        lax.all_gather(out_weight, "dp", axis=0, tiled=True),
        preferred_element_type=jnp.float32,
    ).astype(jnp.bfloat16)


def solution(mesh):
    placed = (
        P("dp", "sp", None, None),
        P("dp", "sp", None, None),
        P("dp", "sp", None, None),
        P("dp", None),
    )
    return jax.shard_map(
        on_device, mesh=mesh, in_specs=placed, out_specs=P("dp", "sp", None), check_vma=False
    )
```

profile of v0, /device:TPU:0, one launch (start us, length us, event | category | flops | bytes accessed | tf_op | source)
XLA Modules:
  0.0 168.0 jit_solution(11725410266001708717)
XLA Ops:
  7.4 0.0 all-reduce.2.cloned.1.call-start
  7.4 9.5 %add_convert_fusion.1 = (bf16[2,1024,16,128]{3,2,1,0:T(8,128)(2,1)}, f32[2,16,128]{2,1,0:T(8,128)S(1)}) fusion(bf16[2,1024,16,128]{3,2,1,0:T(8,128)(2,1)} %param.5), kind=kLoop, calls=%fused_computation.5 | loop fusion | flops 25161728 | bytes 16793600 | tf_op jit(solution)/shard_map/convert_element_type | solution.py:17
  16.8 13.9 %fusion.4 = f32[2,16,128,128]{3,2,1,0:T(8,128)S(1)} fusion(bf16[2,1024,16,128]{3,2,1,0:T(8,128)(2,1)} %param.6, bf16[2,1024,16,128]{3,2,1,0:T(8,128)(2,1)} %get-tuple-element.5), kind=kOutput, calls=%fused_computation.8 | convolution fusion | flops 1073741824 | bytes 18874368 | tf_op jit(solution)/shard_map/bthd,bthe->bhde/dot_general | solution.py:36
  30.8 1.4 pad_maximum_fusion
  32.2 0.0 all-reduce.2.cloned.1.call-update
  32.2 0.2 all-gather.2.cloned.1.call-start
  32.5 0.3 all-gather.2.cloned.1.call-update
  32.8 8.9 %add_convert_fusion = bf16[2,1024,16,128]{3,2,1,0:T(8,128)(2,1)} fusion(bf16[2,1024,16,128]{3,2,1,0:T(8,128)(2,1)} %param.4), kind=kLoop, calls=%fused_computation.3 | loop fusion | flops 16777216 | bytes 16777216 | tf_op jit(solution)/shard_map/convert_element_type | solution.py:17
  41.7 12.6 %copy.16 = bf16[2,1024,16,128]{1,3,2,0:T(8,128)(2,1)} copy(bf16[2,1024,16,128]{3,2,1,0:T(8,128)(2,1)} %add_convert_fusion) | data formatting | bytes 16777216 | tf_op jit(solution)/shard_map/convert_element_type | solution.py:17
  54.3 71.2 %all-reduce.2.cloned.1.call-done = f32[528384]{0:T(1024)} async-done(((f32[528384]{0:T(1024)}), f32[528384]{0:T(1024)}) %all-reduce.2.cloned.1.call-update) | async-done | bytes 2113552 | tf_op jit(solution)/shard_map/psum | solution.py:11
  125.5 0.0 copy-start.1
  125.5 0.9 slice_multiply_fusion.1
  126.4 0.0 copy-start
  126.4 4.7 %fusion.12 = f32[2,16,1,1024]{3,2,1,0:T(1,128)S(1)} fusion(f32[2,16,128,1]{2,3,1,0:T(1,128)S(1)} %bitcast.33, bf16[2,1024,16,128]{1,3,2,0:T(8,128)(2,1)} %copy.16), kind=kOutput, calls=%fused_computation.18 | convolution fusion | flops 8388608 | bytes 8536064 | tf_op jit(solution)/shard_map/bthd,bhd->bth/dot_general | solution.py:29
  131.1 0.0 copy-done.1
  131.1 0.1 fusion.10
  131.3 1.0 copy-done
  132.3 4.5 %fusion.1 = bf16[2,1024,16,128]{1,3,2,0:T(8,128)(2,1)} fusion(f32[2,1024,16]{1,2,0:T(8,128)S(1)} %fusion.11, bf16[2,16,128,128]{3,2,1,0:T(8,128)(2,1)S(1)} %bitcast.32, bf16[2,1024,16,128]{1,3,2,0:T(8,128)(2,1)S(1)} %copy-done), kind=kOutput, calls=%fused_computation.2 | convolution fusion | flops 1086324736 | bytes 17956864 | tf_op jit(solution)/shard_map/bthd,bhde->bthe/dot_general | solution.py:26
  136.8 0.0 all-gather.2.cloned.1.call-done
  136.8 23.7 %fusion.7 = bf16[2,1024,2048]{2,1,0:T(8,128)(2,1)} fusion(bf16[2,1024,2048]{1,2,0:T(8,128)(2,1)} %bitcast.35, bf16[2048,2048]{1,0:T(8,128)(2,1)} %all-gather.2.cloned.1.call-done), kind=kOutput, calls=%fused_computation.11 | convolution fusion | flops 17184063488 | bytes 25165824 | tf_op jit(solution)/shard_map/btw,wv->btv/dot_general | solution.py:44
  (1 shorter events, 0.0 us)
Async XLA Ops:
  7.4 118.1 %all-reduce.2.cloned.1.call-start = ((), (), s32[]{:S(2)}) async-start(), calls=%async_computation | async-start | bytes 4227072 | tf_op jit(solution)/shard_map/psum | solution.py:11
  32.2 104.6 %all-gather.2.cloned.1.call-start = ((), (), s32[]{:S(2)}) async-start(), calls=%async_computation.1 | async-start | bytes 9437184 | tf_op jit(solution)/shard_map/all_gather | solution.py:47
  125.5 5.6 %copy-start.1 = (f32[528384]{0:T(1024)S(1)}, f32[528384]{0:T(1024)}, u32[]{:S(2)}) copy-start(f32[528384]{0:T(1024)} %all-reduce.2.cloned.1.call-done) | copy-start | bytes 6340612
  126.4 5.9 %copy-start = (bf16[2,1024,16,128]{1,3,2,0:T(8,128)(2,1)S(1)}, bf16[2,1024,16,128]{1,3,2,0:T(8,128)(2,1)}, u32[]{:S(2)}) copy-start(bf16[2,1024,16,128]{1,3,2,0:T(8,128)(2,1)} %copy.16) | copy-start | bytes 25165828
Sparse Core Ops, SparseCore 0:
  32.3 93.1 all-reduce.1
Sparse Core Ops, SparseCore 1:
  34.4 52.2 all-gather.1
where the time goes:
time: 168 us
  waiting for transfers between devices  71.5 us (43%)
  matrix products  46.9 us (28%)
  other arithmetic  20.9 us (12%)
  between operations  14.9 us (9%)
  local copies, waits for them, and re-layouts  13.6 us (8%)
    psum x1, waiting for transfers between devices, together(): so_far = lax.psum(jnp.concatenate([a.ravel() for a in arrays]), axis)  71.2 us
    dot_general x1, matrix products, on_device(): jnp.einsum('btw,wv->btv', mixed, lax.all_gather(out_weight, 'dp', axis=0,...  23.7 us
    convert_element_type x2, other arithmetic, feature_map(): return (wide * wide + 0.1).astype(jnp.bfloat16)  18.4 us
    dot_general x1, matrix products, on_device(): jnp.einsum('bthd,bthe->bhde', key_feature, values_in, preferred_element_t...  13.9 us
    convert_element_type x1, local copies, waits for them, and re-layouts, feature_map(): return (wide * wide + 0.1).astype(jnp.bfloat16)  12.6 us
    dot_general x1, matrix products, look_up(): bottom = jnp.einsum('bthd,bhd->bth', features.astype(jnp.float32), mass)  4.72 us
    dot_general x1, matrix products, look_up(): jnp.einsum('bthd,bhde->bthe', features, state.astype(jnp.bfloat16), prefe...  4.55 us
  transfers between devices with their start and end apart: 2, of which 1 were waited for; matrix products, arithmetic and copies ran while one was open for 19% of the time, Pallas kernels for 0%

commit v1 on v0

--- a/solution.py
+++ b/solution.py
@@ -8,7 +8,11 @@
     ends = [0]
     for a in arrays:
         ends.append(ends[-1] + a.size)
-    so_far = lax.psum(jnp.concatenate([a.ravel() for a in arrays]), axis)
+
+    def _meet_rounds(frame, comm_axis):
+        return jnp.sum(jax.lax.all_gather(frame, comm_axis), axis=0)
+
+    so_far = _meet_rounds(jnp.concatenate([a.ravel() for a in arrays]), axis)
     return tuple((so_far[b:e].reshape(a.shape) for a, b, e in zip(arrays, ends, ends[1:])))
 
 

time: 168 us -> 329 us (1.96)
  waiting for transfers between devices: 71.5 us -> 179 us
  local copies, waits for them, and re-layouts: 13.6 us -> 44.3 us
  other arithmetic: 20.9 us -> 44 us
    all_gather x0 -> x1, waiting for transfers between devices: none -> 179 us  [_meet_rounds(): return jnp.sum(jax.lax.all_gather(frame, comm_axis), axis=0)]
    psum x1 -> x0, waiting for transfers between devices: 71.2 us -> none  [together(): so_far = lax.psum(jnp.concatenate([a.ravel() for a in arrays]), axis)]
    all_gather x0 -> x1, local copies, waits for them, and re-layouts: none -> 30.8 us  [_meet_rounds(): return jnp.sum(jax.lax.all_gather(frame, comm_axis), axis=0)]
    reduce_sum x0 -> x1, other arithmetic: none -> 24 us  [_meet_rounds(): return jnp.sum(jax.lax.all_gather(frame, comm_axis), axis=0)]
  transfers between devices with their start and end apart: 2 -> 2, of which waited for: 1 -> 1; matrix products, arithmetic and copies ran while one was open for 19% -> 26% of each run, Pallas kernels for 0% -> 0%
where the time goes in v1:
time: 329 us; the launch traced here: 328 us
  waiting for transfers between devices  179 us (54%)
  matrix products  46.9 us (14%)
  local copies, waits for them, and re-layouts  44.3 us (13%)
  other arithmetic  44 us (13%)
  between operations  13.4 us (4%)
    all_gather x1, waiting for transfers between devices, _meet_rounds(): return jnp.sum(jax.lax.all_gather(frame, comm_axis), axis=0)  179 us
    all_gather x1, local copies, waits for them, and re-layouts, _meet_rounds(): return jnp.sum(jax.lax.all_gather(frame, comm_axis), axis=0)  30.8 us
    reduce_sum x1, other arithmetic, _meet_rounds(): return jnp.sum(jax.lax.all_gather(frame, comm_axis), axis=0)  24 us
    dot_general x1, matrix products, on_device(): jnp.einsum('btw,wv->btv', mixed, lax.all_gather(out_weight, 'dp', axis=0,...  23.7 us
    convert_element_type x2, other arithmetic, feature_map(): return (wide * wide + 0.1).astype(jnp.bfloat16)  18.4 us
    dot_general x1, matrix products, on_device(): jnp.einsum('bthd,bthe->bhde', key_feature, values_in, preferred_element_t...  13.9 us
    convert_element_type x1, local copies, waits for them, and re-layouts, feature_map(): return (wide * wide + 0.1).astype(jnp.bfloat16)  12.6 us
  transfers between devices with their start and end apart: 2, of which 1 were waited for; matrix products, arithmetic and copies ran while one was open for 26% of the time, Pallas kernels for 0%

profile of v1, /device:TPU:0, one launch (start us, length us, event | category | flops | bytes accessed | tf_op | source)
XLA Modules:
  0.0 328.0 jit_solution(7572258202788890514)
XLA Ops:
  6.5 0.0 all-gather.6.cloned.1.call-start
  6.5 9.5 %add_convert_fusion.1 = (bf16[2,1024,16,128]{3,2,1,0:T(8,128)(2,1)}, f32[2,16,128]{2,1,0:T(8,128)S(1)}) fusion(bf16[2,1024,16,128]{3,2,1,0:T(8,128)(2,1)} %param.5), kind=kLoop, calls=%fused_computation.5 | loop fusion | flops 25161728 | bytes 16793600 | tf_op jit(solution)/shard_map/convert_element_type | solution.py:21
  16.0 13.9 %fusion.4 = f32[2,16,128,128]{3,2,1,0:T(8,128)S(1)} fusion(bf16[2,1024,16,128]{3,2,1,0:T(8,128)(2,1)} %param.6, bf16[2,1024,16,128]{3,2,1,0:T(8,128)(2,1)} %get-tuple-element.5), kind=kOutput, calls=%fused_computation.8 | convolution fusion | flops 1073741824 | bytes 18874368 | tf_op jit(solution)/shard_map/bthd,bthe->bhde/dot_general | solution.py:40
  29.9 1.5 pad_maximum_fusion
  31.4 0.0 all-gather.6.cloned.1.call-update
  31.4 0.2 all-gather.4.cloned.1.call-start
  31.6 0.5 all-gather.4.cloned.1.call-update
  32.2 8.9 %add_convert_fusion = bf16[2,1024,16,128]{3,2,1,0:T(8,128)(2,1)} fusion(bf16[2,1024,16,128]{3,2,1,0:T(8,128)(2,1)} %param.4), kind=kLoop, calls=%fused_computation.3 | loop fusion | flops 16777216 | bytes 16777216 | tf_op jit(solution)/shard_map/convert_element_type | solution.py:21
  41.1 12.6 %copy.26 = bf16[2,1024,16,128]{1,3,2,0:T(8,128)(2,1)} copy(bf16[2,1024,16,128]{3,2,1,0:T(8,128)(2,1)} %add_convert_fusion) | data formatting | bytes 16777216 | tf_op jit(solution)/shard_map/convert_element_type | solution.py:21
  53.7 178.5 %all-gather.6.cloned.1.call-done = f32[8454144]{0:T(1024)} async-done(((f32[528384]{0:T(1024)}), f32[8454144]{0:T(1024)}) %all-gather.6.cloned.1.call-update) | async-done | bytes 33816592 | tf_op jit(solution)/shard_map/all_gather | solution.py:13
  232.2 30.8 %reshape.28 = f32[16,528384]{1,0:T(8,128)} reshape(f32[8454144]{0:T(1024)} %all-gather.6.cloned.1.call-done) | data formatting | bytes 67633152 | tf_op jit(solution)/shard_map/all_gather | solution.py:13
  263.0 24.0 %reduce_sum.19 = f32[528384]{0:T(1024)S(1)} reduce(f32[16,528384]{1,0:T(8,128)} %reshape.28, f32[]{:T(128)} %constant.2.clone.1), dimensions={0}, to_apply=%region_1.0 | reduce | flops 7925760 | bytes 35930116 | tf_op jit(solution)/shard_map/reduce_sum | solution.py:13
  287.1 0.0 copy-start
  287.1 4.7 %fusion.12 = f32[2,16,1,1024]{3,2,1,0:T(1,128)S(1)} fusion(f32[2,16,128,1]{2,3,1,0:T(1,128)S(1)} %bitcast.33, bf16[2,1024,16,128]{1,3,2,0:T(8,128)(2,1)} %copy.26), kind=kOutput, calls=%fused_computation.18 | convolution fusion | flops 8388608 | bytes 8536064 | tf_op jit(solution)/shard_map/bthd,bhd->bth/dot_general | solution.py:33
  291.9 0.1 fusion.10
  292.0 0.9 copy-done
  292.9 4.6 %fusion.1 = bf16[2,1024,16,128]{1,3,2,0:T(8,128)(2,1)} fusion(f32[2,1024,16]{1,2,0:T(8,128)S(1)} %fusion.11, bf16[2,16,128,128]{3,2,1,0:T(8,128)(2,1)S(1)} %bitcast.32, bf16[2,1024,16,128]{1,3,2,0:T(8,128)(2,1)S(1)} %copy-done), kind=kOutput, calls=%fused_computation.2 | convolution fusion | flops 1086324736 | bytes 17956864 | tf_op jit(solution)/shard_map/bthd,bhde->bthe/dot_general | solution.py:30
  297.4 0.0 all-gather.4.cloned.1.call-done
  297.4 23.7 %fusion.7 = bf16[2,1024,2048]{2,1,0:T(8,128)(2,1)} fusion(bf16[2,1024,2048]{1,2,0:T(8,128)(2,1)} %bitcast.35, bf16[2048,2048]{1,0:T(8,128)(2,1)} %all-gather.4.cloned.1.call-done), kind=kOutput, calls=%fused_computation.11 | convolution fusion | flops 17184063488 | bytes 25165824 | tf_op jit(solution)/shard_map/btw,wv->btv/dot_general | solution.py:48
  (2 shorter events, 0.0 us)
Async XLA Ops:
  6.5 225.7 %all-gather.6.cloned.1.call-start = ((), (), s32[]{:S(2)}) async-start(), calls=%async_computation.1 | async-start | bytes 35930112 | tf_op jit(solution)/shard_map/all_gather | solution.py:13
  31.4 266.0 %all-gather.4.cloned.1.call-start = ((), (), s32[]{:S(2)}) async-start(), calls=%async_computation | async-start | bytes 9437184 | tf_op jit(solution)/shard_map/all_gather | solution.py:51
  287.1 5.8 %copy-start = (bf16[2,1024,16,128]{1,3,2,0:T(8,128)(2,1)S(1)}, bf16[2,1024,16,128]{1,3,2,0:T(8,128)(2,1)}, u32[]{:S(2)}) copy-start(bf16[2,1024,16,128]{1,3,2,0:T(8,128)(2,1)} %copy.26) | copy-start | bytes 25165828
Sparse Core Ops, SparseCore 0:
  31.5 200.6 all-gather.5
  234.0 49.5 all-gather.3
